TPU v7x, 256 devices: a whole 4x4x8 slice. The times are simulated.
256 devices in a mesh: patch: 32 (over x, z_hi, core), tp: 8 (over y, z_lo).
Axes of the slice: x: 4, y: 4, z: 8 (z_hi: 4, z_lo: 2; z = z_hi * 2 + z_lo), core: 2. Of those that a mesh axis runs over, the one named last changes fastest.
Arguments:
- resid_corrupt: bfloat16 [512, 4096], P(None, 'tp'), may hold values from -6 to 6
- resid_clean: bfloat16 [2, 512, 4096], P(None, 'patch', 'tp'), may hold values from -6 to 6
- patch_level: int32 [32], P('patch'), may hold values from 0 to 1
- patch_mask: int32 [32, 128], P('patch'), may hold values 0 or 1
- norm_gain: bfloat16 [4096], P('tp'), may hold values from 0.099609375 to 1.8984375
- final_gain: bfloat16 [4096], P('tp'), may hold values from 0.099609375 to 1.8984375
- w_query: bfloat16 [4096, 4096], P('patch', 'tp'), may hold values from -1 to 1
- w_key: bfloat16 [4096, 1024], P('patch', 'tp'), may hold values from -1 to 1
- w_value: bfloat16 [4096, 1024], P('patch', 'tp'), may hold values from -0.09375 to 0.09375
- w_out: bfloat16 [4096, 4096], P('tp', 'patch'), may hold values from -0.09375 to 0.09375
- unembed: bfloat16 [128256, 4096], P(('patch', 'tp')), may hold values from -0.09375 to 0.09375
- scored_ids: int32 [256], replicated, may hold values from 0 to 128255
- base_logits: float32 [512, 256], P('tp'), may hold values from -6 to 6
Outputs:
- logit_shift: float32 [32, 512, 256], P('patch', 'tp')
All inputs are finite; a program needn't handle non-finite values. No bound on the sum of `patch_mask` on one device may be relied on, other than what follows from the above.
Results may differ from a plain program's by a relative error of at most 0.01.
The roundings to bfloat16 on the way count: a program that leaves them out, or rounds other values in their place, can miss the bound.
Values may be sent and summed in bfloat16 or wider, within the bound.
A program may use at most 128 MiB of HBM per device.

v0:
```python
import jax
import jax.numpy as jnp
from jax import lax
from jax.sharding import PartitionSpec as P

D = 4096
HD = 128
SEQ = 128
PROMPTS = 4
EPSILON = 1e-05
THETA = 500000.0


def in_one_piece(arrays, axis, dim, along):
    both = jnp.concatenate(arrays, axis=along)
    out, at, gathered = (lax.all_gather(both, axis, axis=dim, tiled=True), 0, [])
    for a in arrays:
        gathered.append(lax.slice_in_dim(out, at, at + a.shape[along], axis=along))
        at += a.shape[along]
    return tuple(gathered)


def in_blocks(value, dim, peers):
    dims = value.shape
    pieces = value.reshape(*dims[:dim], peers, dims[dim] // peers, *dims[dim + 1 :])
    return jnp.moveaxis(pieces, dim, 0)


def summed_on_arrival(value, axis, dim):
    pieces = in_blocks(value, dim, lax.axis_size(axis))
    arrived = lax.all_to_all(pieces, axis, split_axis=0, concat_axis=0, tiled=True)
    return arrived.astype(jnp.float32).sum(axis=0)


def total_of_pieces(value, axis):
    pieces = lax.all_gather(value, axis).astype(jnp.float32)
    return pieces.sum(axis=0)


def rope_tables(length, head_dim):
    half = head_dim // 2
    freqs = THETA ** (-(jnp.arange(half, dtype=jnp.float32) * 2.0 / head_dim))
    angles = jnp.arange(length, dtype=jnp.float32)[:, None] * freqs[None, :]
    return (jnp.cos(angles)[:, None, :], jnp.sin(angles)[:, None, :])


def rotate(values, cosine, sine):
    half = values.shape[-1] // 2
    lower = values[..., :half]
    upper = values[..., half:]
    return jnp.concatenate([lower * cosine - upper * sine, upper * cosine + lower * sine], axis=-1)


def rms_scale(rows, gain):
    return rows * lax.rsqrt(jnp.mean(rows * rows, axis=-1, keepdims=True) + EPSILON) * gain


def attend(query_f, key_f, value_f):
    heads = query_f.shape[1] // HD
    kv_heads = key_f.shape[1] // HD
    group = heads // kv_heads
    prompts = query_f.shape[0] // SEQ
    cosine, sine = rope_tables(SEQ, HD)
    queries = rotate(query_f.reshape(prompts, SEQ, heads, HD), cosine, sine).astype(jnp.bfloat16)
    queries = queries.reshape(prompts, SEQ, kv_heads, group, HD)
    key_rows = rotate(key_f.reshape(prompts, SEQ, kv_heads, HD), cosine, sine).astype(jnp.bfloat16)
    value_rows = value_f.astype(jnp.bfloat16).reshape(prompts, SEQ, kv_heads, HD)
    scores = jnp.einsum(
        "pqkgd,pskd->pkgqs", queries, key_rows, preferred_element_type=jnp.float32
    ) * HD ** (-0.5)
    causal = lax.iota(jnp.int32, SEQ)[:, None] >= lax.iota(jnp.int32, SEQ)[None, :]
    scores = jnp.where(causal, scores, -1e30)
    probs = jax.nn.softmax(scores, axis=-1).astype(jnp.bfloat16)
    attended = jnp.einsum(
        "pkgqs,pskd->pqkgd", probs, value_rows, preferred_element_type=jnp.float32
    )
    return attended.astype(jnp.bfloat16).reshape(prompts * SEQ, heads * HD)


def on_device(
    resid_corrupt,
    resid_clean,
    patch_level,
    patch_mask,
    norm_gain,
    final_gain,
    w_query,
    w_key,
    w_value,
    w_out,
    unembed,
    scored_ids,
    base_logits,
):
    level = patch_level[0]
    row_mask = jnp.tile(patch_mask[0], PROMPTS) == 1
    clean_all = lax.all_gather(resid_clean, "patch", axis=1, tiled=True)
    early = (row_mask & (level == 0))[:, None]
    layer_in = jnp.where(early, clean_all[0], resid_corrupt)
    full_rows, full_gain = (
        lax.all_gather(layer_in, "tp", axis=1, tiled=True),
        lax.all_gather(norm_gain, "tp", axis=0, tiled=True),
    )
    normed = rms_scale(full_rows.astype(jnp.float32), full_gain.astype(jnp.float32)).astype(
        jnp.bfloat16
    )
    pieces = in_one_piece((w_query, w_key, w_value), "patch", 0, 1)
    query_f = jnp.dot(normed, pieces[0], preferred_element_type=jnp.float32)
    key_f = jnp.dot(normed, pieces[1], preferred_element_type=jnp.float32)
    value_f = jnp.dot(normed, pieces[2], preferred_element_type=jnp.float32)
    attended = attend(query_f, key_f, value_f)
    partial_out = jnp.dot(
        attended,
        lax.all_gather(w_out, "patch", axis=1, tiled=True),
        preferred_element_type=jnp.float32,
    )
    head_block = summed_on_arrival(partial_out.astype(jnp.bfloat16), "tp", 1)
    middle = layer_in.astype(jnp.float32) + head_block
    late = (row_mask & (level == 1))[:, None]
    residual = jnp.where(late, clean_all[1].astype(jnp.float32), middle)
    squares = lax.psum(jnp.sum(residual * residual, axis=1), "tp")
    scaling = lax.rsqrt(squares / D + EPSILON)[:, None]
    final_block = (residual * scaling * final_gain.astype(jnp.float32)).astype(jnp.bfloat16)
    rows_dev = unembed.shape[0]
    first_row = lax.axis_index(("patch", "tp")) * rows_dev
    owned_rows = (scored_ids[:, None] == first_row + lax.iota(jnp.int32, rows_dev)[None, :]).astype(
        jnp.bfloat16
    )
    picked = jnp.dot(owned_rows, unembed, preferred_element_type=jnp.float32)
    spread = summed_on_arrival(picked.astype(jnp.bfloat16), "tp", 1)
    score_block = (
        total_of_pieces(spread.astype(jnp.bfloat16), "patch")
        .astype(jnp.float32)
        .astype(jnp.bfloat16)
    )
    partial_logits = jnp.einsum(
        "td,sd->ts", final_block, score_block, preferred_element_type=jnp.float32
    )
    token_logits = summed_on_arrival(partial_logits.astype(jnp.bfloat16), "tp", 0)
    return (token_logits - base_logits)[None]


def solution(mesh):
    placed = (
        P(None, "tp"),
        P(None, "patch", "tp"),
        P("patch"),
        P("patch", None),
        P("tp"),
        P("tp"),
        P("patch", "tp"),
        P("patch", "tp"),
        P("patch", "tp"),
        P("tp", "patch"),
        P(("patch", "tp"), None),
        P(),
        P("tp", None),
    )
    return jax.shard_map(
        on_device, mesh=mesh, in_specs=placed, out_specs=P("patch", "tp", None), check_vma=False
    )
```

profile of v0, /device:TPU:2, one launch (start us, length us, event | category | flops | bytes accessed | tf_op | source)
XLA Modules:
  0.0 461.8 jit_solution(4920440208380993172)
XLA Ops:
  6.5 0.7 all-gather.8.cloned.1.call-update
  8.0 0.7 and_bitcast_fusion.1
  8.6 55.1 %all-gather.8.cloned.1.call-done = bf16[2,512,512]{2,1,0:T(8,128)(2,1)} async-done(((bf16[2,16,512]{2,1,0:T(8,128)(2,1)}), bf16[2,512,512]{2,1,0:T(8,128)(2,1)}) %all-gather.8.cloned.1.call-update) | async-done | bytes 1048592 | tf_op jit(solution)/shard_map/all_gather | solution.py:97
  63.7 2.1 fusion.14
  65.9 1.7 pad_maximum_fusion
  67.6 0.5 all-gather.14.cloned.1.call-update
  68.2 3.5 convolution_convert_fusion.1
  72.0 54.5 %all_to_all.15 = bf16[8,256,512]{2,1,0:T(8,128)(2,1)S(1)} all-to-all(bf16[8,256,512]{2,1,0:T(8,128)(2,1)S(1)} %bitcast.85), channel_id=1, replica_groups=mesh['patch'=32,'tp'=8] {'tp'}, dimensions={0} | all-to-all | bytes 4194304 | tf_op jit(solution)/shard_map/all_to_all | solution.py:31
  126.5 1.1 reduce_sum.73
  127.6 25.7 %all-gather.1 = bf16[8,1,512]{2,1,0:T(2,128)(2,1)S(1)} all-gather(bf16[1,1,512]{2,1,0:T(2,128)(2,1)S(1)} %reshape.154), channel_id=1, replica_groups=mesh['patch'=32,'tp'=8] {'tp'}, dimensions={0}, use_global_device_ids=true | all-gather | bytes 9216 | tf_op jit(solution)/shard_map/all_gather | solution.py:102
  153.6 27.4 %all-gather.10.cloned.1.call-done = bf16[512,4096]{1,0:T(8,128)(2,1)} async-done(((bf16[512,512]{1,0:T(8,128)(2,1)}), bf16[512,4096]{1,0:T(8,128)(2,1)}) %all-gather.10.cloned.1.call-update) | async-done | bytes 4194320 | tf_op jit(solution)/shard_map/all_gather | solution.py:101
  181.0 3.1 fusion
  184.1 67.0 %all-gather.12.cloned.1.call-done = bf16[4096,768]{1,0:T(8,128)(2,1)} async-done(((bf16[128,768]{1,0:T(8,128)(2,1)}), bf16[4096,768]{1,0:T(8,128)(2,1)}) %all-gather.12.cloned.1.call-update) | async-done | bytes 6291472 | tf_op jit(solution)/shard_map/all_gather | solution.py:16
  251.1 5.8 %fusion.3 = f32[512,512]{1,0:T(8,128)S(1)} fusion(bf16[4096,768]{1,0:T(8,128)(2,1)} %all-gather.12.cloned.1.call-done, bf16[512,4096]{1,0:T(8,128)(2,1)} %all-gather.10.cloned.1.call-done, f32[4096]{0:T(1024)S(1)} %bitcast.91, f32[512]{0:T(512)S(1)} %add_rsqrt_fusion.1), kind=kOutput, calls=%fused_computation.9 | convolution fusion | flops 2155872256 | bytes 9455616 | tf_op jit(solution)/shard_map/dot_general | solution.py:108
  257.0 0.4 reshape.146
  257.3 3.8 fusion.8
  261.3 0.6 fusion.34
  262.2 0.5 fusion.35
  262.9 1.2 copy-done.1
  264.1 2.6 convolution_convert_fusion.4
  267.4 48.2 %all-gather.14.cloned.1.call-done = bf16[512,4096]{1,0:T(8,128)(2,1)} async-done(((bf16[512,128]{1,0:T(8,128)(2,1)}), bf16[512,4096]{1,0:T(8,128)(2,1)}) %all-gather.14.cloned.1.call-update) | async-done | bytes 4194320 | tf_op jit(solution)/shard_map/all_gather | solution.py:114
  315.5 4.5 convolution_convert_fusion
  320.1 2.3 copy.57
  322.4 5.0 %all-to-all-start = ((bf16[8,512,512]{2,1,0:T(8,128)(2,1)}), bf16[8,512,512]{2,1,0:T(8,128)(2,1)}, u32[]{:S(2)}, u32[]{:S(2)}) async-start(bf16[8,512,512]{2,1,0:T(8,128)(2,1)} %bitcast.83), calls=%async_computation | async-start | bytes 8388608 | tf_op jit(solution)/shard_map/all_to_all | solution.py:31
  327.4 92.0 %all-to-all-done = bf16[8,512,512]{2,1,0:T(8,128)(2,1)} async-done(((bf16[8,512,512]{2,1,0:T(8,128)(2,1)}), bf16[8,512,512]{2,1,0:T(8,128)(2,1)}, u32[]{:S(2)}, u32[]{:S(2)}) %all-to-all-start) | async-done | bytes 4194336 | tf_op jit(solution)/shard_map/all_to_all | solution.py:31
  419.5 2.9 convert_reduce_fusion
  422.4 0.4 multiply_reduce_fusion
  422.7 16.9 %psum.7 = f32[512]{0:T(512)S(1)} all-reduce(f32[512]{0:T(512)S(1)} %multiply_reduce_fusion), channel_id=1, replica_groups=mesh['patch'=32,'tp'=8] {'tp'}, use_global_device_ids=true, to_apply=%region_5.6 | all-reduce | flops 512 | bytes 4096 | tf_op jit(solution)/shard_map/psum | solution.py:121
  439.6 4.8 %reduce_sum.74 = bf16[256,512]{1,0:T(8,128)(2,1)S(1)} reduce(bf16[32,256,512]{2,1,0:T(8,128)(2,1)} %bitcast.84, bf16[]{:T(256)} %constant.47.clone.1), dimensions={0}, to_apply=%region_7.8 | reduce | flops 4063232 | bytes 8650754 | tf_op jit(solution)/shard_map/reduce_sum | solution.py:37
  444.4 0.4 convolution_convert_fusion.3
  444.9 9.7 %all_to_all.16 = bf16[8,64,256]{2,1,0:T(8,128)(2,1)S(1)} all-to-all(bf16[8,64,256]{2,1,0:T(8,128)(2,1)S(1)} %bitcast.90), channel_id=1, replica_groups=mesh['patch'=32,'tp'=8] {'tp'}, dimensions={0} | all-to-all | bytes 524288 | tf_op jit(solution)/shard_map/all_to_all | solution.py:31
  454.6 0.6 subtract_bitcast_fusion
  (38 shorter events, 2.1 us)
Async XLA Ops:
  6.5 57.2 %all-gather.8.cloned.1.call-start = ((), (), s32[]{:S(2)}) async-start(), calls=%async_computation.3 | async-start | bytes 1081344 | tf_op jit(solution)/shard_map/all_gather | solution.py:97
  7.3 173.8 %all-gather.10.cloned.1.call-start = ((), (), s32[]{:S(2)}) async-start(), calls=%async_computation.4 | async-start | bytes 4718592 | tf_op jit(solution)/shard_map/all_gather | solution.py:101
  65.9 185.3 %all-gather.12.cloned.1.call-start = ((), (), s32[]{:S(2)}) async-start(), calls=%async_computation.5 | async-start | bytes 6488064 | tf_op jit(solution)/shard_map/all_gather | solution.py:16
  67.6 247.9 %all-gather.14.cloned.1.call-start = ((), (), s32[]{:S(2)}) async-start(), calls=%async_computation.6 | async-start | bytes 4325376 | tf_op jit(solution)/shard_map/all_gather | solution.py:114
  68.2 371.4 %all-gather.16.cloned.1.call-start = ((), (), s32[]{:S(2)}) async-start(), calls=%async_computation.7 | async-start | bytes 8650752 | tf_op jit(solution)/shard_map/all_gather | solution.py:36
  72.0 55.6 %copy-start.4 = (bf16[512]{0:T(512)(128)(2,1)S(1)}, bf16[512]{0:T(512)(128)(2,1)}, u32[]{:S(2)}) copy-start(bf16[512]{0:T(512)(128)(2,1)} %param.17) | copy-start | bytes 3076
  261.9 2.2 copy-start.1
  322.4 5.0 %copy-start.5 = (bf16[512]{0:T(512)(128)(2,1)S(1)}, bf16[512]{0:T(512)(128)(2,1)}, u32[]{:S(2)}) copy-start(bf16[512]{0:T(512)(128)(2,1)} %param.18) | copy-start | bytes 3076
  322.4 97.0 %all-to-all-start = ((bf16[8,512,512]{2,1,0:T(8,128)(2,1)}), bf16[8,512,512]{2,1,0:T(8,128)(2,1)}, u32[]{:S(2)}, u32[]{:S(2)}) async-start(bf16[8,512,512]{2,1,0:T(8,128)(2,1)} %bitcast.83), calls=%async_computation | async-start | bytes 8388608 | tf_op jit(solution)/shard_map/all_to_all | solution.py:31
  327.4 94.9 %copy-start = (bf16[512,512]{1,0:T(8,128)(2,1)S(1)}, bf16[512,512]{1,0:T(8,128)(2,1)}, u32[]{:S(2)}) copy-start(bf16[512,512]{1,0:T(8,128)(2,1)} %fusion.14) | copy-start | bytes 1572868
  327.4 94.9 %copy-start.2 = (bf16[2,512,512]{2,1,0:T(8,128)(2,1)S(1)}, bf16[2,512,512]{2,1,0:T(8,128)(2,1)}, u32[]{:S(2)}) copy-start(bf16[2,512,512]{2,1,0:T(8,128)(2,1)} %all-gather.8.cloned.1.call-done) | copy-start | bytes 3145732
  439.6 15.0 %copy-start.3 = (f32[64,256]{1,0:T(8,128)S(1)}, f32[64,256]{1,0:T(8,128)}, u32[]{:S(2)}) copy-start(f32[64,256]{1,0:T(8,128)} %param.25) | copy-start | bytes 196612
Sparse Core Ops, SparseCore 0:
  10.0 53.6 all-gather.7
  66.0 115.0 all-gather.9
  183.6 67.4 all-gather.11
  253.4 62.0 all-gather.13
  317.9 95.5 all-gather.15
where the time goes:
time: 462 us
  waiting for transfers between devices  291 us (63%)
  blocking collectives  107 us (23%)
  matrix products  21.6 us (5%)
  other arithmetic  18.2 us (4%)
  between operations  14 us (3%)
  starting transfers between devices  5.12 us (1%)
  local copies, waits for them, and re-layouts  5.11 us (1%)
    all_to_all x1, waiting for transfers between devices, summed_on_arrival(): lax.all_to_all(pieces, axis, split_axis=0, concat_axis=0, tiled=True)  92 us
    all_gather x1, waiting for transfers between devices, in_one_piece(): lax.all_gather(both, axis, axis=dim, tiled=True)  67 us
    all_to_all x2, blocking collectives, summed_on_arrival(): lax.all_to_all(pieces, axis, split_axis=0, concat_axis=0, tiled=True)  64.2 us
    all_gather x1, waiting for transfers between devices, on_device(): clean_all = lax.all_gather(resid_clean, 'patch', axis=1, tiled=True)  55.1 us
    all_gather x1, waiting for transfers between devices, on_device(): lax.all_gather(w_out, 'patch', axis=1, tiled=True)  48.2 us
    all_gather x1, waiting for transfers between devices, on_device(): lax.all_gather(layer_in, 'tp', axis=1, tiled=True)  27.4 us
    all_gather x1, blocking collectives, on_device(): lax.all_gather(norm_gain, 'tp', axis=0, tiled=True)  25.7 us
    psum x1, blocking collectives, on_device(): squares = lax.psum(jnp.sum(residual * residual, axis=1), 'tp')  16.9 us
  transfers between devices with their start and end apart: 6, of which 5 were waited for; matrix products, arithmetic and copies ran while one was open for 8% of the time, Pallas kernels for 0%

commit v1 on v0

--- a/solution.py
+++ b/solution.py
@@ -97,8 +97,20 @@
     clean_all = lax.all_gather(resid_clean, "patch", axis=1, tiled=True)
     early = (row_mask & (level == 0))[:, None]
     layer_in = jnp.where(early, clean_all[0], resid_corrupt)
+
+    def matrix_time(local_array, peer_axis):
+        return jnp.concatenate(
+            jax.lax.all_to_all(
+                jnp.stack([local_array for _ in range(jax.lax.axis_size(peer_axis))]),
+                peer_axis,
+                split_axis=0,
+                concat_axis=0,
+            ),
+            axis=1,
+        )
+
     full_rows, full_gain = (
-        lax.all_gather(layer_in, "tp", axis=1, tiled=True),
+        matrix_time(layer_in, "tp"),
         lax.all_gather(norm_gain, "tp", axis=0, tiled=True),
     )
     normed = rms_scale(full_rows.astype(jnp.float32), full_gain.astype(jnp.float32)).astype(

time: 462 us -> 372 us (0.81)
  waiting for transfers between devices: 291 us -> 122 us
  local copies, waits for them, and re-layouts: 5.11 us -> 48.1 us
  blocking collectives: 107 us -> 124 us
  other arithmetic: 18.2 us -> 28.8 us
  starting transfers between devices: 5.12 us -> 15.6 us
    all_gather x1, blocking collectives: 25.7 us -> 97.5 us  [on_device(): lax.all_gather(norm_gain, 'tp', axis=0, tiled=True)]
    all_gather x1, waiting for transfers between devices: 67 us -> 0.01 us  [in_one_piece(): lax.all_gather(both, axis, axis=dim, tiled=True)]
    all_to_all x2 -> x1, blocking collectives: 64.2 us -> 10.1 us  [summed_on_arrival(): lax.all_to_all(pieces, axis, split_axis=0, concat_axis=0, tiled=True)]
    all_gather x1, waiting for transfers between devices: 48.2 us -> 0.02 us  [on_device(): lax.all_gather(w_out, 'patch', axis=1, tiled=True)]
    all_gather x1 -> x0, waiting for transfers between devices: 27.4 us -> none  [on_device(): lax.all_gather(layer_in, 'tp', axis=1, tiled=True)]
    convert_element_type x0 -> x3, local copies, waits for them, and re-layouts: none -> 27 us  [the longest x2 20 us: on_device(): full_rows.astype(jnp.float32)]
    all_gather x1, waiting for transfers between devices: 55.1 us -> 40.6 us  [on_device(): clean_all = lax.all_gather(resid_clean, 'patch', axis=1, tiled=True)]
    all_to_all x1 -> x2, waiting for transfers between devices: 92 us -> 80.1 us  [summed_on_arrival(): lax.all_to_all(pieces, axis, split_axis=0, concat_axis=0, tiled=True)]
  transfers between devices with their start and end apart: 6 -> 7, of which waited for: 5 -> 2; matrix products, arithmetic and copies ran while one was open for 8% -> 23% of each run, Pallas kernels for 0% -> 0%
where the time goes in v1:
time: 372 us; the launch traced here: 371 us
  blocking collectives  124 us (33%)
  waiting for transfers between devices  122 us (33%)
  local copies, waits for them, and re-layouts  48.1 us (13%)
  other arithmetic  28.8 us (8%)
  matrix products  18 us (5%)
  starting transfers between devices  15.6 us (4%)
  between operations  14.1 us (4%)
    all_gather x1, blocking collectives, on_device(): lax.all_gather(norm_gain, 'tp', axis=0, tiled=True)  97.5 us
    all_to_all x2, waiting for transfers between devices, summed_on_arrival(): lax.all_to_all(pieces, axis, split_axis=0, concat_axis=0, tiled=True)  80.1 us
    all_gather x1, waiting for transfers between devices, on_device(): clean_all = lax.all_gather(resid_clean, 'patch', axis=1, tiled=True)  40.6 us
    convert_element_type x2, local copies, waits for them, and re-layouts, on_device(): full_rows.astype(jnp.float32)  20 us
    psum x1, blocking collectives, on_device(): squares = lax.psum(jnp.sum(residual * residual, axis=1), 'tp')  16.3 us
    all_to_all x2, starting transfers between devices, summed_on_arrival(): lax.all_to_all(pieces, axis, split_axis=0, concat_axis=0, tiled=True)  10.8 us
    all_to_all x1, blocking collectives, summed_on_arrival(): lax.all_to_all(pieces, axis, split_axis=0, concat_axis=0, tiled=True)  10.1 us
    unnamed x25, local copies, waits for them, and re-layouts  7.94 us
  transfers between devices with their start and end apart: 7, of which 2 were waited for; matrix products, arithmetic and copies ran while one was open for 23% of the time, Pallas kernels for 0%

profile of v1, /device:TPU:2, one launch (start us, length us, event | category | flops | bytes accessed | tf_op | source)
XLA Modules:
  0.0 370.8 jit_solution(13818816652168625694)
XLA Ops:
  7.3 1.0 copy.53
  9.2 0.9 copy.55
  10.8 3.5 convolution_convert_fusion.1
  14.4 1.5 copy.92
  15.9 5.8 %all-to-all-start.2 = ((bf16[8,256,512]{2,1,0:T(8,128)(2,1)}), bf16[8,256,512]{2,1,0:T(8,128)(2,1)S(1)}, u32[]{:S(2)}, u32[]{:S(2)}) async-start(bf16[8,256,512]{2,1,0:T(8,128)(2,1)} %bitcast.117), calls=%async_computation.2 | async-start | bytes 4194304 | tf_op jit(solution)/shard_map/all_to_all | solution.py:31
  23.2 40.6 %all-gather.7.cloned.1.call-done = bf16[2,512,512]{2,1,0:T(8,128)(2,1)} async-done(((bf16[2,16,512]{2,1,0:T(8,128)(2,1)}), bf16[2,512,512]{2,1,0:T(8,128)(2,1)}) %all-gather.7.cloned.1.call-update) | async-done | bytes 1048592 | tf_op jit(solution)/shard_map/all_gather | solution.py:97
  63.8 1.2 fusion.16
  65.0 2.3 stack.2
  67.3 4.7 %all-to-all-start = ((bf16[8,512,512]{2,1,0:T(8,128)(2,1)}), bf16[8,512,512]{2,1,0:T(8,128)(2,1)}, u32[]{:S(2)}, u32[]{:S(2)}) async-start(bf16[8,512,512]{2,1,0:T(8,128)(2,1)} %stack.2), calls=%async_computation | async-start | bytes 8388608 | tf_op jit(solution)/shard_map/all_to_all | solution.py:103
  72.1 1.0 reduce_sum.73
  73.2 97.5 %all-gather.1 = bf16[8,1,512]{2,1,0:T(2,128)(2,1)S(1)} all-gather(bf16[1,1,512]{2,1,0:T(2,128)(2,1)S(1)} %reshape.207), channel_id=1, replica_groups=mesh['patch'=32,'tp'=8] {'tp'}, dimensions={0}, use_global_device_ids=true | all-gather | bytes 9216 | tf_op jit(solution)/shard_map/all_gather | solution.py:114
  170.9 6.6 %copy.52 = bf16[8,512,512]{1,2,0:T(8,128)(2,1)} copy(bf16[8,512,512]{2,1,0:T(8,128)(2,1)} %all-to-all-done) | data formatting | bytes 8388608 | tf_op jit(solution)/shard_map/all_to_all | solution.py:103
  177.6 6.6 %convert_bitcast_fusion = f32[512,8,512]{0,2,1:T(8,128)} fusion(bf16[8,512,512]{1,2,0:T(8,128)(2,1)} %copy.52), kind=kLoop, calls=%fused_computation.7 | loop fusion | flops 2097152 | bytes 12582912 | tf_op jit(solution)/shard_map/convert_element_type | solution.py:116
  184.1 9.9 %reshape.216 = f32[4,128,4096]{1,0,2:T(4,128)} reshape(f32[512,8,512]{0,2,1:T(8,128)} %convert_bitcast_fusion) | data formatting | bytes 16777216 | tf_op jit(solution)/shard_map/convert_element_type | solution.py:116
  194.1 10.1 %copy.72 = f32[4,128,4096]{2,1,0:T(8,128)} copy(f32[4,128,4096]{1,0,2:T(4,128)} %reshape.216) | data formatting | bytes 16777216 | tf_op jit(solution)/shard_map/convert_element_type | solution.py:116
  204.2 3.3 multiply_reduce_fusion
  207.6 2.6 fusion.3
  210.2 7.0 %reshape.217 = bf16[4,128,4096]{1,0,2:T(4,128)(2,1)} reshape(bf16[512,8,512]{0,2,1:T(8,128)(2,1)} %fusion.3) | data formatting | bytes 8388608 | tf_op jit(solution)/shard_map/convert_element_type | solution.py:116
  217.1 4.2 %fusion.1 = bf16[512,4096]{0,1:T(8,128)(2,1)} fusion(bf16[8,512,512]{1,2,0:T(8,128)(2,1)} %copy.52, f32[4096]{0:T(1024)S(1)} %bitcast.124, f32[512]{0:T(512)S(1)} %get-tuple-element.10), kind=kLoop, calls=%fused_computation.2 | loop fusion | flops 8388608 | bytes 8407040 | tf_op jit(solution)/shard_map/convert_element_type | solution.py:116
  221.3 2.8 copy-done.1
  224.1 5.2 %fusion.11 = f32[4,128,1,128]{1,3,0,2:T(8,128)S(1)} fusion(f32[4,128,4096]{2,1,0:T(8,128)} %copy.72, f32[4096]{0:T(1024)S(1)} %bitcast.125, f32[4,128]{1,0:T(4,128)S(1)} %get-tuple-element.9, bf16[4096,768]{0,1:T(8,128)(2,1)S(1)} %copy-done.1), kind=kOutput, calls=%fused_computation.24 | convolution fusion | flops 543162368 | bytes 9717760 | tf_op jit(solution)/shard_map/dot_general | solution.py:121
  229.9 2.3 fusion.4
  233.0 1.6 copy-done.2
  234.6 1.3 convolution_convert_fusion.4
  236.6 4.5 %convolution_convert_fusion = bf16[512,4096]{1,0:T(8,128)(2,1)S(1)} fusion(bf16[512,4096]{1,0:T(8,128)(2,1)} %all-gather.11.cloned.1.call-done, bf16[64,8,4,128]{3,2,1,0:T(4,128)(2,1)S(1)} %bitcast.122), kind=kOutput, calls=%fused_computation.8 | convolution fusion | flops 2149580800 | bytes 8912896 | tf_op jit(solution)/shard_map/dot_general | solution.py:124
  241.1 2.3 copy.91
  243.5 5.0 %all-to-all-start.1 = ((bf16[8,512,512]{2,1,0:T(8,128)(2,1)}), bf16[8,512,512]{2,1,0:T(8,128)(2,1)}, u32[]{:S(2)}, u32[]{:S(2)}) async-start(bf16[8,512,512]{2,1,0:T(8,128)(2,1)} %bitcast.115), calls=%async_computation.1 | async-start | bytes 8388608 | tf_op jit(solution)/shard_map/all_to_all | solution.py:31
  248.5 80.1 %all-to-all-done.1 = bf16[8,512,512]{2,1,0:T(8,128)(2,1)} async-done(((bf16[8,512,512]{2,1,0:T(8,128)(2,1)}), bf16[8,512,512]{2,1,0:T(8,128)(2,1)}, u32[]{:S(2)}, u32[]{:S(2)}) %all-to-all-start.1) | async-done | bytes 4194336 | tf_op jit(solution)/shard_map/all_to_all | solution.py:31
  328.6 2.9 convert_reduce_fusion
  331.9 16.3 %psum.7 = f32[512]{0:T(512)S(1)} all-reduce(f32[512]{0:T(512)S(1)} %multiply_reduce_fusion.1), channel_id=1, replica_groups=mesh['patch'=32,'tp'=8] {'tp'}, use_global_device_ids=true, to_apply=%region_5.6 | all-reduce | flops 512 | bytes 4096 | tf_op jit(solution)/shard_map/psum | solution.py:133
  348.2 4.8 %reduce_sum.74 = bf16[256,512]{1,0:T(8,128)(2,1)S(1)} reduce(bf16[32,256,512]{2,1,0:T(8,128)(2,1)} %bitcast.116, bf16[]{:T(256)} %constant.47.clone.1), dimensions={0}, to_apply=%region_7.8 | reduce | flops 4063232 | bytes 8650754 | tf_op jit(solution)/shard_map/reduce_sum | solution.py:37
  353.5 10.1 %all_to_all.20 = bf16[8,64,256]{2,1,0:T(8,128)(2,1)S(1)} all-to-all(bf16[8,64,256]{2,1,0:T(8,128)(2,1)S(1)} %bitcast.123), channel_id=1, replica_groups=mesh['patch'=32,'tp'=8] {'tp'}, dimensions={0} | all-to-all | bytes 524288 | tf_op jit(solution)/shard_map/all_to_all | solution.py:31
  (58 shorter events, 7.1 us)
Async XLA Ops:
  6.5 57.3 %all-gather.7.cloned.1.call-start = ((), (), s32[]{:S(2)}) async-start(), calls=%async_computation.4 | async-start | bytes 1081344 | tf_op jit(solution)/shard_map/all_gather | solution.py:97
  7.3 214.0 %all-gather.9.cloned.1.call-start = ((), (), s32[]{:S(2)}) async-start(), calls=%async_computation.5 | async-start | bytes 6488064 | tf_op jit(solution)/shard_map/all_gather | solution.py:16
  14.4 8.8 %copy-start.9 = (s32[1,128]{1,0:T(1,128)S(1)}, s32[1,128]{1,0:T(1,128)}, u32[]{:S(2)}) copy-start(s32[1,128]{1,0:T(1,128)} %param.16) | copy-start | bytes 1540
  14.4 49.4 %copy-start.5 = (bf16[512,512]{1,0:T(8,128)(2,1)S(1)}, bf16[512,512]{1,0:T(8,128)(2,1)}, u32[]{:S(2)}) copy-start(bf16[512,512]{1,0:T(8,128)(2,1)} %param.13) | copy-start | bytes 1572868
  15.9 49.1 %all-to-all-start.2 = ((bf16[8,256,512]{2,1,0:T(8,128)(2,1)}), bf16[8,256,512]{2,1,0:T(8,128)(2,1)S(1)}, u32[]{:S(2)}, u32[]{:S(2)}) async-start(bf16[8,256,512]{2,1,0:T(8,128)(2,1)} %bitcast.117), calls=%async_computation.2 | async-start | bytes 4194304 | tf_op jit(solution)/shard_map/all_to_all | solution.py:31
  21.7 214.8 %all-gather.11.cloned.1.call-start = ((), (), s32[]{:S(2)}) async-start(), calls=%async_computation.6 | async-start | bytes 4325376 | tf_op jit(solution)/shard_map/all_gather | solution.py:126
  67.3 5.9 %copy-start.7 = (bf16[512]{0:T(512)(128)(2,1)S(1)}, bf16[512]{0:T(512)(128)(2,1)}, u32[]{:S(2)}) copy-start(bf16[512]{0:T(512)(128)(2,1)} %param.17) | copy-start | bytes 3076
  67.3 103.6 %all-to-all-start = ((bf16[8,512,512]{2,1,0:T(8,128)(2,1)}), bf16[8,512,512]{2,1,0:T(8,128)(2,1)}, u32[]{:S(2)}, u32[]{:S(2)}) async-start(bf16[8,512,512]{2,1,0:T(8,128)(2,1)} %stack.2), calls=%async_computation | async-start | bytes 8388608 | tf_op jit(solution)/shard_map/all_to_all | solution.py:103
  72.0 276.2 %all-gather.13.cloned.1.call-start = ((), (), s32[]{:S(2)}) async-start(), calls=%async_computation.7 | async-start | bytes 8650752 | tf_op jit(solution)/shard_map/all_gather | solution.py:36
  204.2 3.4 copy-start
  221.3 2.8 copy-start.1
  224.1 5.2 %slice-start = ((bf16[4096,768]{0,1:T(8,128)(2,1)}), bf16[4096,512]{0,1:T(8,128)(2,1)S(1)}, s32[]{:S(2)}) async-start(bf16[4096,768]{0,1:T(8,128)(2,1)} %all-gather.9.cloned.1.call-done), calls=%async_computation.8 | async-start | bytes 8388608 | tf_op jit(solution)/shard_map/slice | solution.py:18
  224.1 5.9 %copy-start.3 = (bf16[4,128,4096]{1,0,2:T(4,128)(2,1)S(1)}, bf16[4,128,4096]{1,0,2:T(4,128)(2,1)}, u32[]{:S(2)}) copy-start(bf16[4,128,4096]{1,0,2:T(4,128)(2,1)} %reshape.217) | copy-start | bytes 12582916
  232.3 2.3 copy-start.2
  243.5 5.0 %copy-start.8 = (bf16[512]{0:T(512)(128)(2,1)S(1)}, bf16[512]{0:T(512)(128)(2,1)}, u32[]{:S(2)}) copy-start(bf16[512]{0:T(512)(128)(2,1)} %param.18) | copy-start | bytes 3076
  243.5 85.1 %all-to-all-start.1 = ((bf16[8,512,512]{2,1,0:T(8,128)(2,1)}), bf16[8,512,512]{2,1,0:T(8,128)(2,1)}, u32[]{:S(2)}, u32[]{:S(2)}) async-start(bf16[8,512,512]{2,1,0:T(8,128)(2,1)} %bitcast.115), calls=%async_computation.1 | async-start | bytes 8388608 | tf_op jit(solution)/shard_map/all_to_all | solution.py:31
  248.5 83.0 %copy-start.4 = (bf16[2,512,512]{2,1,0:T(8,128)(2,1)S(1)}, bf16[2,512,512]{2,1,0:T(8,128)(2,1)}, u32[]{:S(2)}) copy-start(bf16[2,512,512]{2,1,0:T(8,128)(2,1)} %all-gather.7.cloned.1.call-done) | copy-start | bytes 3145732
  348.2 15.3 %copy-start.6 = (f32[64,256]{1,0:T(8,128)S(1)}, f32[64,256]{1,0:T(8,128)}, u32[]{:S(2)}) copy-start(f32[64,256]{1,0:T(8,128)} %param.25) | copy-start | bytes 196612
Sparse Core Ops, SparseCore 0:
  10.0 53.7 all-gather.6
  66.3 88.6 all-gather.8
  157.4 62.6 all-gather.10
  222.5 93.1 all-gather.12
